TPU v7x, 512 devices: a whole 4x8x8 slice. The times are simulated.
512 devices in a mesh: grp: 4 (over x), row: 16 (over z, core), col: 8 (over y).
Axes of the slice: x: 4, y: 8, z: 8, core: 2. Of those that a mesh axis runs over, the one named last changes fastest.
Arguments:
- fields: bfloat16 [4, 4, 768, 6144], P('grp', None, 'row', 'col'), may hold values from -12 to 12
- offset: int32 [1], replicated, may hold values from 0 to 767
- level_index: int32 [4], replicated, may hold values from 0 to 3, each once
- nudge_rate: float32 [4], replicated, may hold values from 0.2 to 0.9
- driving: float32 [4, 64, 64], replicated, may hold values from -4 to 4
Outputs:
- nudged: bfloat16 [4, 4, 768, 6144], P('grp', None, 'row', 'col')
Inputs may be any that keep to these rules, and one draw needn't show every extreme that they name: `offset`: the footprint covers a third of the parent rows from there on, wrapping around the periodic domain. `level_index`: each parent level is fed by exactly one child level.
All inputs are finite; a program needn't handle non-finite values.
Results may differ from a plain program's by a relative error of at most 0.0034.
Values may be sent and summed in bfloat16 or wider, within the bound.
A program may use at most 64 MiB of HBM per device.

v0:
```python
import math

import jax
import jax.numpy as jnp
from jax import lax
from jax.sharding import Mesh
from jax.sharding import PartitionSpec as P

MAX_WAVE = 32
ROW = ("row_0", "row_1")


def joined_along(blocks, dim):
    blocks = jnp.moveaxis(blocks, 0, dim)
    lengths = blocks.shape
    return blocks.reshape(*lengths[:dim], lengths[dim] * lengths[dim + 1], *lengths[dim + 2 :])


def sent_to_all(shard, axis):
    peers = lax.axis_size(axis)
    return lax.all_to_all(
        jnp.broadcast_to(shard[None], (peers, *shard.shape)), axis, 0, 0, tiled=True
    )


def gathered_copies(shard, axis, dim):
    return joined_along(sent_to_all(shard, axis), dim)


def cut_along(shard, dim, peers):
    lengths = shard.shape
    blocks = shard.reshape(*lengths[:dim], peers, lengths[dim] // peers, *lengths[dim + 1 :])
    return jnp.moveaxis(blocks, dim, 0)


def sent_and_summed(shard, axis, dim):
    peers = lax.axis_size(axis)
    blocks = lax.all_to_all(cut_along(shard, dim, peers), axis, 0, 0, tiled=True)
    return jnp.sum(blocks, axis=0)


def summed_rows(shard, axes, dim):
    far, near = axes
    blocks = cut_along(shard, dim, lax.axis_size(far))
    nearer = sent_and_summed(blocks, near, dim + 1)
    arrived = lax.all_to_all(nearer, far, split_axis=0, concat_axis=0, tiled=True)
    return arrived.sum(axis=0)


def padded_to(lines, peers):
    spare = -len(lines) % peers
    return jnp.pad(lines, [(0, spare)] + [(0, 0)] * (lines.ndim - 1))


def gather_axes(shard, axes, dim):
    far, near = axes
    blocks = sent_to_all(sent_to_all(shard, far), near)
    return joined_along(blocks.swapaxes(0, 1).reshape(-1, *shard.shape), dim)


def sum_by_parts(shard, axes):
    lines = shard.reshape(-1)
    own = summed_rows(padded_to(lines, lax.axis_size(axes[0]) * lax.axis_size(axes[1])), axes, 0)
    whole = gather_axes(own, axes, 0)
    return whole[: len(lines)].reshape(shard.shape)


def fourier_table(positions, cell_count, max_order):
    orders = jnp.arange(1, max_order + 1, dtype=jnp.int32)
    period = 3 * cell_count
    phase_index = positions[:, None] * orders[None, :] % period
    angles = phase_index.astype(jnp.float32) * jnp.float32(2.0 * math.pi / period)
    wave_scale = jnp.float32(math.sqrt(2.0 / cell_count))
    constant = jnp.full((positions.shape[0], 1), 1.0 / math.sqrt(cell_count), jnp.float32)
    return jnp.concatenate(
        [constant, wave_scale * jnp.cos(angles), wave_scale * jnp.sin(angles[:, : max_order - 1])],
        axis=1,
    )


def place_rows(carried, block_rows, strip_index):
    height = block_rows.shape[1]
    inside = (strip_index >= 0) & (strip_index < height)
    picked = jnp.take(block_rows, jnp.clip(strip_index, 0, height - 1), axis=1)
    mask_shape = (1, inside.shape[0]) + (1,) * (block_rows.ndim - 2)
    return jnp.where(inside.reshape(mask_shape), picked, carried)


def per_device(fields, offset, level_index, nudge_rate, driving):
    group_id = lax.axis_index("grp")
    row_id = lax.axis_index(ROW)
    col_id = lax.axis_index("col")
    group_count = lax.axis_size("grp")
    local_slab = fields[0]
    levels, tile_rows, tile_cols = local_slab.shape
    full_rows = lax.axis_size(ROW) * tile_rows
    full_cols = lax.axis_size("col") * tile_cols
    third_rows = tile_rows // 3
    third_cols = tile_cols // 3
    shift_rows = offset[0]
    is_parent = group_id == group_count - 1
    level_ids = jnp.arange(levels, dtype=jnp.int32)
    inverse = jnp.sum(
        level_ids[:, None] * (level_index[:, None] == level_ids[None, :]).astype(jnp.int32), axis=0
    )
    parent_rows = row_id * tile_rows + jnp.arange(tile_rows, dtype=jnp.int32)
    parent_cols = col_id * tile_cols + jnp.arange(tile_cols, dtype=jnp.int32)
    strip_index = (parent_rows - shift_rows) % full_rows
    covered = strip_index < full_rows // 3
    row_table = fourier_table(3 * parent_rows, full_rows, MAX_WAVE)
    col_table = fourier_table(3 * parent_cols, full_cols, MAX_WAVE)
    row_half = lax.optimization_barrier(row_table.astype(jnp.bfloat16))
    row_rounded = row_half.astype(jnp.float32)
    col_rounded = col_table.astype(jnp.bfloat16)
    block_sums = jnp.sum(
        local_slab.reshape(levels, third_rows, 3, third_cols, 3), axis=(2, 4), dtype=jnp.float32
    )
    averaged = (block_sums / 9.0).astype(jnp.bfloat16)
    by_parent = jnp.take(averaged, inverse, axis=0)
    empty_tile = jnp.zeros((levels, tile_rows, third_cols), jnp.bfloat16)
    placed = place_rows(empty_tile, gathered_copies(by_parent, ROW, 1), strip_index)
    thirds = gathered_copies(placed[:, :, None, :], "grp", 2)
    arrived = thirds[:, :, : group_count - 1, :].reshape(levels, tile_rows, tile_cols)
    fed_tile = jnp.where(covered[None, :, None], arrived, local_slab)
    projected = jnp.einsum("lrc,cm->lrm", fed_tile, col_rounded, preferred_element_type=jnp.float32)
    partial_sums = jnp.einsum(
        "rn,lrm->lnm", row_rounded, projected, precision=lax.Precision.HIGHEST
    )
    coeffs = sum_by_parts(
        jnp.where(is_parent, partial_sums, jnp.zeros_like(partial_sums)),
        (("grp", "row_0"), ("row_1", "col")),
    )
    amplitude = math.sqrt(full_rows * full_cols) / (2 * MAX_WAVE)
    deficit = amplitude * driving - coeffs
    child_rows = (3 * shift_rows + parent_rows - 1) % (3 * full_rows)
    child_cols = (
        (3 * col_id + group_id) * tile_cols + jnp.arange(tile_cols, dtype=jnp.int32) - 1
    ) % (3 * full_cols)
    rows_used = jnp.where(is_parent, row_table, fourier_table(child_rows, full_rows, MAX_WAVE))
    cols_used = jnp.where(is_parent, col_table, fourier_table(child_cols, full_cols, MAX_WAVE))
    level_deficit = jnp.where(is_parent, deficit, jnp.take(deficit, level_index, axis=0))
    level_rate = jnp.where(is_parent, nudge_rate, jnp.take(nudge_rate, level_index, axis=0))
    base_tile = jnp.where(is_parent, fed_tile, local_slab)
    spread_cols = jnp.einsum(
        "lnm,cm->lnc", level_deficit, cols_used, precision=lax.Precision.HIGHEST
    )
    increment = jnp.einsum("rn,lnc->lrc", rows_used, spread_cols, precision=lax.Precision.HIGHEST)
    result = (base_tile.astype(jnp.float32) + level_rate[:, None, None] * increment).astype(
        jnp.bfloat16
    )
    return result[None]


def solution(mesh):
    torus = Mesh(
        mesh.devices.reshape(mesh.shape["grp"], 8, 2, mesh.shape["col"]),
        ("grp", "row_0", "row_1", "col"),
    )
    in_specs = (P("grp", None, ROW, "col"), P(), P(), P(), P())
    out_specs = P("grp", None, ROW, "col")
    return jax.shard_map(
        per_device, mesh=torus, in_specs=in_specs, out_specs=out_specs, check_vma=False
    )
```

profile of v0, /device:TPU:1, one launch (start us, length us, event | category | flops | bytes accessed | tf_op | source)
XLA Modules:
  0.0 146.2 jit_solution(10059725681167154296)
XLA Ops:
  0.0 0.7 select_reduce_fusion
  0.8 0.0 copy-start.1
  0.8 0.0 copy-start.3
  0.8 0.0 copy-start
  0.8 25.9 %reshape.155 = f32[4,16,3,256,3]{4,3,2,1,0:T(8,128)} reshape(bf16[1,4,48,768]{3,2,1,0:T(8,128)(2,1)} %param.5) | data formatting | bytes 884736 | tf_op jit(solution)/shard_map/convert_element_type | solution.py:115
  26.7 0.0 copy-start.2
  26.7 11.8 %reduce_sum.39 = f32[4,16,256]{2,1,0:T(8,128)S(1)} reduce(f32[4,16,3,256,3]{4,3,2,1,0:T(8,128)} %reshape.155, f32[]{:T(128)} %constant.147.clone.1), dimensions={2,4}, to_apply=%region_1.2 | reduce | flops 131072 | bytes 655364 | tf_op jit(solution)/shard_map/reduce_sum | solution.py:115
  38.6 0.5 gather_fusion
  39.1 0.1 broadcast_select_fusion
  39.2 0.8 broadcast_in_dim.102
  40.0 11.8 %all-to-all-start = ((bf16[16,4,16,256]{3,2,1,0:T(8,128)(2,1)}), bf16[16,4,16,256]{3,2,1,0:T(8,128)(2,1)S(1)}, u32[]{:S(2)}, u32[]{:S(2)}) async-start(bf16[16,4,16,256]{3,2,1,0:T(8,128)(2,1)} %broadcast_in_dim.102), calls=%async_computation | async-start | bytes 1048576 | tf_op jit(solution)/shard_map/all_to_all | solution.py:21
  52.6 0.3 cosine_multiply_fusion.2
  52.8 0.1 fusion.40
  53.0 0.1 fusion.55
  53.1 0.1 fusion.39
  53.2 0.8 cosine_multiply_fusion.1
  54.1 15.0 %all-to-all-done = bf16[16,4,16,256]{3,2,1,0:T(8,128)(2,1)S(1)} async-done(((bf16[16,4,16,256]{3,2,1,0:T(8,128)(2,1)}), bf16[16,4,16,256]{3,2,1,0:T(8,128)(2,1)S(1)}, u32[]{:S(2)}, u32[]{:S(2)}) %all-to-all-start) | async-done | bytes 524320 | tf_op jit(solution)/shard_map/all_to_all | solution.py:21
  69.1 0.4 copy.17
  69.5 0.7 gather_fusion.1
  70.2 0.2 select_bitcast_fusion
  70.4 0.8 broadcast_in_dim.105
  71.2 4.0 %all-to-all-start.1 = ((bf16[4,4,48,1,256]{4,2,1,3,0:T(8,128)(2,1)}), bf16[4,4,48,1,256]{4,2,1,3,0:T(8,128)(2,1)S(1)}, u32[]{:S(2)}, u32[]{:S(2)}) async-start(bf16[4,4,48,1,256]{4,2,1,3,0:T(8,128)(2,1)} %broadcast_in_dim.105), calls=%async_computation.1 | async-start | bytes 786432 | tf_op jit(solution)/shard_map/all_to_all | solution.py:21
  75.2 0.6 fusion.21
  75.9 7.2 %all-to-all-done.1 = bf16[4,4,48,1,256]{4,2,1,3,0:T(8,128)(2,1)S(1)} async-done(((bf16[4,4,48,1,256]{4,2,1,3,0:T(8,128)(2,1)}), bf16[4,4,48,1,256]{4,2,1,3,0:T(8,128)(2,1)S(1)}, u32[]{:S(2)}, u32[]{:S(2)}) %all-to-all-start.1) | async-done | bytes 393248 | tf_op jit(solution)/shard_map/all_to_all | solution.py:21
  83.2 0.0 copy-done.1
  83.2 0.3 fusion.14
  83.5 0.3 fusion.4
  83.8 0.1 copy.20
  83.9 0.1 reshape_reshape.3
  84.0 0.1 copy.21
  84.1 0.8 reshape.196
  84.9 7.4 %all-to-all-start.2 = ((f32[16,1,1024]{2,1,0:T(1,128)}), f32[16,1,1024]{2,1,0:T(1,128)S(1)}, u32[]{:S(2)}, u32[]{:S(2)}) async-start(f32[16,1,1024]{2,1,0:T(1,128)} %reshape.196), calls=%async_computation.2 | async-start | bytes 131072 | tf_op jit(solution)/shard_map/all_to_all | solution.py:38
  92.3 0.0 copy-done.3
  92.3 7.1 %all-to-all-done.2 = f32[16,1,1024]{2,1,0:T(1,128)S(1)} async-done(((f32[16,1,1024]{2,1,0:T(1,128)}), f32[16,1,1024]{2,1,0:T(1,128)S(1)}, u32[]{:S(2)}, u32[]{:S(2)}) %all-to-all-start.2) | async-done | bytes 65568 | tf_op jit(solution)/shard_map/all_to_all | solution.py:38
  99.4 0.5 broadcast.446
  99.9 0.8 reduce.1
  100.7 0.1 reshape.197
  100.8 0.6 reduce_sum.41
  101.4 4.1 %all-to-all-start.3 = ((f32[32,1,32]{2,1,0:T(1,128)}), f32[32,1,32]{2,1,0:T(1,128)S(1)}, u32[]{:S(2)}, u32[]{:S(2)}) async-start(f32[32,1,32]{2,1,0:T(1,128)} %bitcast.14), calls=%async_computation.3 | async-start | bytes 32768 | tf_op jit(solution)/shard_map/all_to_all | solution.py:46
  105.6 0.0 copy-done
  105.6 0.6 gather_fusion.2
  106.3 7.9 %all-to-all-done.3 = f32[32,1,32]{2,1,0:T(1,128)S(1)} async-done(((f32[32,1,32]{2,1,0:T(1,128)}), f32[32,1,32]{2,1,0:T(1,128)S(1)}, u32[]{:S(2)}, u32[]{:S(2)}) %all-to-all-start.3) | async-done | bytes 4128 | tf_op jit(solution)/shard_map/all_to_all | solution.py:46
  114.2 0.1 reduce_sum.42
  114.2 0.6 broadcast_in_dim.108
  114.9 3.8 %all-to-all-start.4 = ((f32[32,1,32]{2,1,0:T(1,128)}), f32[32,1,32]{2,1,0:T(1,128)S(1)}, u32[]{:S(2)}, u32[]{:S(2)}) async-start(f32[32,1,32]{2,1,0:T(1,128)} %broadcast_in_dim.108), calls=%async_computation.4 | async-start | bytes 32768 | tf_op jit(solution)/shard_map/all_to_all | solution.py:21
  118.7 8.6 %all-to-all-done.4 = f32[32,1,32]{2,1,0:T(1,128)S(1)} async-done(((f32[32,1,32]{2,1,0:T(1,128)}), f32[32,1,32]{2,1,0:T(1,128)S(1)}, u32[]{:S(2)}, u32[]{:S(2)}) %all-to-all-start.4) | async-done | bytes 4128 | tf_op jit(solution)/shard_map/all_to_all | solution.py:21
  127.3 0.8 reshape.198
  128.1 6.8 %all-to-all-start.5 = ((f32[16,1,1024]{2,1,0:T(1,128)}), f32[16,1,1024]{2,1,0:T(1,128)S(1)}, u32[]{:S(2)}, u32[]{:S(2)}) async-start(f32[16,1,1024]{2,1,0:T(1,128)} %reshape.198), calls=%async_computation.5 | async-start | bytes 131072 | tf_op jit(solution)/shard_map/all_to_all | solution.py:21
  134.9 7.2 %all-to-all-done.5 = f32[16,1,1024]{2,1,0:T(1,128)S(1)} async-done(((f32[16,1,1024]{2,1,0:T(1,128)}), f32[16,1,1024]{2,1,0:T(1,128)S(1)}, u32[]{:S(2)}, u32[]{:S(2)}) %all-to-all-start.5) | async-done | bytes 65568 | tf_op jit(solution)/shard_map/all_to_all | solution.py:21
  142.1 0.8 reduce.2
  142.9 0.1 reshape.199
  143.0 0.2 copy.22
  143.1 0.1 reshape_reshape_reshape.3
  143.2 0.0 copy-done.2
  143.3 0.6 gather_fusion.3
  143.8 0.9 fusion.6
  144.7 1.5 %fusion.3 = bf16[1,4,48,768]{3,2,1,0:T(8,128)(2,1)} fusion(f32[4,64,768]{2,1,0:T(8,128)S(1)} %fusion.6, bf16[1,4,48,768]{3,2,1,0:T(8,128)(2,1)S(1)} %copy-done.1, f32[4]{0:T(128)S(1)} %broadcast_select_fusion.1, pred[]{:T(512)S(6)} %eq.27, bf16[4,48,768]{2,1,0:T(8,128)(2,1)S(1)} %bitcast.67, pred[48]{0:T(512)(128)(4,1)S(1)} %broadcast_compare_fusion, ...), kind=kOutput, calls=%fused_computation.8 | convolution fusion | flops 114146304 | bytes 1695681 | tf_op jit(solution)/shard_map/rn,lnc->lrc/dot_general | solution.py:147
  (24 shorter events, 0.3 us)
Async XLA Ops:
  0.8 82.4 %copy-start.1 = (bf16[1,4,48,768]{3,2,1,0:T(8,128)(2,1)S(1)}, bf16[1,4,48,768]{3,2,1,0:T(8,128)(2,1)}, u32[]{:S(2)}) copy-start(bf16[1,4,48,768]{3,2,1,0:T(8,128)(2,1)} %param.5) | copy-start | bytes 884740
  0.8 91.5 %copy-start.3 = (s32[4]{0:T(128)S(1)}, s32[4]{0:T(128)}, u32[]{:S(2)}) copy-start(s32[4]{0:T(128)} %param.7) | copy-start | bytes 52
  0.8 104.8 %copy-start = (f32[4]{0:T(128)S(1)}, f32[4]{0:T(128)}, u32[]{:S(2)}) copy-start(f32[4]{0:T(128)} %param.8) | copy-start | bytes 52
  26.7 116.5 %copy-start.2 = (f32[4,64,64]{2,1,0:T(8,128)S(1)}, f32[4,64,64]{2,1,0:T(8,128)}, u32[]{:S(2)}) copy-start(f32[4,64,64]{2,1,0:T(8,128)} %param.9) | copy-start | bytes 196612
  40.0 29.0 %all-to-all-start = ((bf16[16,4,16,256]{3,2,1,0:T(8,128)(2,1)}), bf16[16,4,16,256]{3,2,1,0:T(8,128)(2,1)S(1)}, u32[]{:S(2)}, u32[]{:S(2)}) async-start(bf16[16,4,16,256]{3,2,1,0:T(8,128)(2,1)} %broadcast_in_dim.102), calls=%async_computation | async-start | bytes 1048576 | tf_op jit(solution)/shard_map/all_to_all | solution.py:21
  71.2 11.9 %all-to-all-start.1 = ((bf16[4,4,48,1,256]{4,2,1,3,0:T(8,128)(2,1)}), bf16[4,4,48,1,256]{4,2,1,3,0:T(8,128)(2,1)S(1)}, u32[]{:S(2)}, u32[]{:S(2)}) async-start(bf16[4,4,48,1,256]{4,2,1,3,0:T(8,128)(2,1)} %broadcast_in_dim.105), calls=%async_computation.1 | async-start | bytes 786432 | tf_op jit(solution)/shard_map/all_to_all | solution.py:21
  84.9 14.5 %all-to-all-start.2 = ((f32[16,1,1024]{2,1,0:T(1,128)}), f32[16,1,1024]{2,1,0:T(1,128)S(1)}, u32[]{:S(2)}, u32[]{:S(2)}) async-start(f32[16,1,1024]{2,1,0:T(1,128)} %reshape.196), calls=%async_computation.2 | async-start | bytes 131072 | tf_op jit(solution)/shard_map/all_to_all | solution.py:38
  101.4 12.7 %all-to-all-start.3 = ((f32[32,1,32]{2,1,0:T(1,128)}), f32[32,1,32]{2,1,0:T(1,128)S(1)}, u32[]{:S(2)}, u32[]{:S(2)}) async-start(f32[32,1,32]{2,1,0:T(1,128)} %bitcast.14), calls=%async_computation.3 | async-start | bytes 32768 | tf_op jit(solution)/shard_map/all_to_all | solution.py:46
  114.9 12.4 %all-to-all-start.4 = ((f32[32,1,32]{2,1,0:T(1,128)}), f32[32,1,32]{2,1,0:T(1,128)S(1)}, u32[]{:S(2)}, u32[]{:S(2)}) async-start(f32[32,1,32]{2,1,0:T(1,128)} %broadcast_in_dim.108), calls=%async_computation.4 | async-start | bytes 32768 | tf_op jit(solution)/shard_map/all_to_all | solution.py:21
  128.1 14.0 %all-to-all-start.5 = ((f32[16,1,1024]{2,1,0:T(1,128)}), f32[16,1,1024]{2,1,0:T(1,128)S(1)}, u32[]{:S(2)}, u32[]{:S(2)}) async-start(f32[16,1,1024]{2,1,0:T(1,128)} %reshape.198), calls=%async_computation.5 | async-start | bytes 131072 | tf_op jit(solution)/shard_map/all_to_all | solution.py:21
where the time goes:
time: 147 us; the launch traced here: 146 us
  waiting for transfers between devices  53 us (36%)
  starting transfers between devices  38 us (26%)
  local copies, waits for them, and re-layouts  34 us (23%)
  other arithmetic  17.2 us (12%)
  matrix products  2.96 us (2%)
    all_to_all x4, waiting for transfers between devices, sent_to_all(): lax.all_to_all(jnp.broadcast_to(shard[None], (peers, *shard.shape)), axis...  38 us
    all_to_all x4, starting transfers between devices, sent_to_all(): lax.all_to_all(jnp.broadcast_to(shard[None], (peers, *shard.shape)), axis...  26.5 us
    convert_element_type x1, local copies, waits for them, and re-layouts, per_device(): jnp.sum(local_slab.reshape(levels, third_rows, 3, third_cols, 3), axis=(2...  25.9 us
    reduce_sum x1, other arithmetic, per_device(): jnp.sum(local_slab.reshape(levels, third_rows, 3, third_cols, 3), axis=(2...  11.8 us
    all_to_all x1, waiting for transfers between devices, summed_rows(): lax.all_to_all(nearer, far, split_axis=0, concat_axis=0, tiled=True)  7.93 us
    all_to_all x1, starting transfers between devices, sent_and_summed(): lax.all_to_all(cut_along(shard, dim, peers), axis, 0, 0, tiled=True)  7.38 us
    all_to_all x1, waiting for transfers between devices, sent_and_summed(): lax.all_to_all(cut_along(shard, dim, peers), axis, 0, 0, tiled=True)  7.11 us
    all_to_all x1, starting transfers between devices, summed_rows(): lax.all_to_all(nearer, far, split_axis=0, concat_axis=0, tiled=True)  4.15 us
  transfers between devices with their start and end apart: 6, of which 6 were waited for; matrix products, arithmetic and copies ran while one was open for 2% of the time, Pallas kernels for 0%

commit v1 on v0

v1 whole, which is shorter than its diff:
```python
import math

import jax
import jax.numpy as jnp
from jax import lax
from jax.experimental import pallas as pl
from jax.experimental.pallas import tpu as pltpu
from jax.sharding import PartitionSpec as P

MESH = pl.DeviceIdType.MESH
F32 = jnp.float32
BF16 = jnp.bfloat16
I32 = jnp.int32

L = 4
W = 32
B = 64
ROWS = 768
COLS = 6144
TR = 48
TC = 768
NX = 4
NY = 8
NZ = 8
NR = 16


def iota(shape, dim):
    return lax.broadcasted_iota(I32, shape, dim)


def basis(m, z, cells):
    period = 3 * cells
    wave = jnp.where(m <= W, m, m - W).astype(F32)
    shift = jnp.where(m <= W, 0.0, period / 4).astype(F32)
    scale = jnp.where(m == 0, 1.0 / math.sqrt(cells), math.sqrt(2.0 / cells)).astype(F32)
    phase = wave * z.astype(F32) - shift
    phase = phase - period * jnp.floor(phase * (1.0 / period))
    t = (jnp.abs(phase - period / 2) - period / 4) * (2.0 * math.pi / period)
    s = t * t
    acc = F32(1.0 / math.factorial(13))
    for k in (11, 9, 7, 5, 3, 1):
        sign = -1.0 if k in (11, 7, 3) else 1.0
        acc = acc * s + F32(sign / math.factorial(k))
    return scale * (t * acc)


def split(v):
    hi = v.astype(BF16)
    return hi, (v - hi.astype(F32)).astype(BF16)


def dot(a, b):
    return jnp.dot(a, b, preferred_element_type=F32)


def dot_nt(a, b):
    return lax.dot_general(a, b, (((1,), (1,)), ((), ())), preferred_element_type=F32)


def bytes_wait(ref, sem):
    pltpu.make_async_copy(ref, ref, sem).wait()


def kernel(
    x_hbm, off_ref, lev_ref, rate_ref, drv_ref, out_ref,
    x_ref, pool_ref, sums_ref, avg_ref, own_ref, colt_ref, part_ref, rs_ref, ysrc_ref, y_ref,
    zsrc_ref, z_ref, all_ref, gat_ref, win_ref, fed_ref, drvp_ref, rows3_ref, chi_ref, clo_ref,
    in_sem, rs_send, rs_recv, y_send, y_recv, z_send, z_recv, ag_send, ag_recv,
    g_send, g_recv, w_send, w_recv,
):
    grp = lax.axis_index("grp")
    row = lax.axis_index("row")
    col = lax.axis_index("col")
    zed = row // 2
    core = row % 2
    seat = grp * 2 + core
    is_parent = grp == NX - 1
    off = off_ref[0]

    load = pltpu.make_async_copy(x_hbm, x_ref, in_sem)
    load.start()

    barrier = pltpu.get_barrier_semaphore()

    def seat_peer(d):
        other = (seat + d) % 8
        return other, (other // 2, zed * 2 + other % 2, col)

    def y_peer(d):
        return (grp, row, (col + d) % NY)

    def z_peer(d):
        return (grp, ((zed + d) % NZ) * 2 + core, col)

    def greet(dev):
        pl.semaphore_signal(barrier, inc=1, device_id=dev, device_id_type=MESH)

    for d in range(1, 8):
        greet(seat_peer(d)[1])
        greet(y_peer(d))
        greet(z_peer(d))

    @pl.when(jnp.logical_not(is_parent))
    def _():
        for d in range(1, 8):
            greet((grp, ((zed + d) % NZ) * 2 + 1 - core, col))

    @pl.when(jnp.logical_not(is_parent))
    def _():
        j = iota((TC, 256), 0)
        t = iota((TC, 256), 1) * 3
        pool_ref[...] = jnp.where((j >= t) & (j < t + 3), 1.0, 0.0).astype(BF16)
        xs = 3 * (col * TC + grp * 256 + iota((B, 256), 1))
        colt_ref[:, :256] = basis(iota((B, 256), 0), xs, COLS).astype(BF16)

    @pl.when(is_parent)
    def _():
        xs = 3 * (col * TC + iota((B, TC), 1))
        colt_ref[...] = basis(iota((B, TC), 0), xs, COLS).astype(BF16)

    load.wait()

    def add_part(rowt, proj, rows):
        for pair in range(2):
            lo = 2 * pair * rows
            both = jnp.concatenate([proj[lo : lo + rows], proj[lo + rows : lo + 2 * rows]], axis=1)
            hi, low = split(both)
            part = dot(rowt, hi) + dot(rowt, low)
            part_ref[4 * pair : 4 * pair + 4] = part.reshape(4, 16, 128)

    @pl.when(jnp.logical_not(is_parent))
    def _():
        xs = x_ref[...].reshape(L * TR, TC)
        for h in range(2):
            cut = slice(128 * h, 128 * h + 128)
            sums_ref[h] = dot(xs, pool_ref[:, cut])
            total = (
                sums_ref[h, pl.ds(0, 64, stride=3), :]
                + sums_ref[h, pl.ds(1, 64, stride=3), :]
                + sums_ref[h, pl.ds(2, 64, stride=3), :]
            )
            avg_ref[:, :, cut] = (total / 9.0).reshape(L, 16, 128)
        for p in range(L):
            inv = jnp.int32(0)
            for l in range(1, L):
                inv = jnp.where(lev_ref[l] == p, l, inv)
            own_ref[p] = avg_ref[inv].astype(BF16)
        proj = dot_nt(own_ref[...].reshape(64, 256), colt_ref[:, :256])
        rr = off + 16 * row + iota((B, 16), 1)
        rowt = basis(iota((B, 16), 0), 3 * rr, ROWS).astype(BF16)
        add_part(rowt, proj, 16)

    @pl.when(is_parent)
    def _():
        proj = dot_nt(x_ref[...].reshape(L * TR, TC), colt_ref[...])
        rr = TR * row + iota((B, TR), 1)
        s = rr - off
        s = jnp.where(s < 0, s + ROWS, s)
        rowt = basis(iota((B, TR), 0), 3 * rr, ROWS)
        rowt = jnp.where(s < ROWS // 3, 0.0, rowt).astype(BF16)
        add_part(rowt, proj, TR)

    pl.semaphore_wait(barrier, jnp.where(is_parent, 21, 28))

    for d in range(1, 8):
        other, dev = seat_peer(d)
        pltpu.make_async_remote_copy(
            src_ref=part_ref.at[other], dst_ref=rs_ref.at[d - 1], send_sem=rs_send, recv_sem=rs_recv,
            device_id=dev, device_id_type=MESH,
        ).start()

    @pl.when(jnp.logical_not(is_parent))
    def _():
        for d in range(1, NR):
            other = (row + d) % NR
            pltpu.make_async_remote_copy(
                src_ref=own_ref.at[pl.ds(2 * (other % 2), 2)], dst_ref=gat_ref.at[row],
                send_sem=g_send, recv_sem=g_recv, device_id=(grp, other, col), device_id_type=MESH,
            ).start()
        gat_ref[row] = own_ref[pl.ds(2 * core, 2)]

    for pair in range(2):
        both = jnp.concatenate([drv_ref[2 * pair], drv_ref[2 * pair + 1]], axis=1)
        drvp_ref[4 * pair : 4 * pair + 4] = (
            both * (math.sqrt(ROWS * COLS) / (2 * W))
        ).reshape(4, 16, 128)
    t = iota((TR, B), 0)
    zr = jnp.where(is_parent, 3 * (TR * row + t), 3 * off + TR * row + t - 1)
    hi, low = split(basis(iota((TR, B), 1), zr, ROWS))
    rows3_ref[...] = jnp.concatenate([hi, hi, low], axis=1)

    bytes_wait(rs_ref, rs_recv)
    total = part_ref[seat]
    for d in range(7):
        total = total + rs_ref[d]
    ysrc_ref[...] = total
    for d in range(1, NY):
        pltpu.make_async_remote_copy(
            src_ref=ysrc_ref, dst_ref=y_ref.at[d - 1], send_sem=y_send, recv_sem=y_recv,
            device_id=y_peer(d), device_id_type=MESH,
        ).start()

    for n in range(3):
        t = iota((B, 256), 1) + 256 * n
        zc = jnp.where(is_parent, 3 * (col * TC + t), (3 * col + grp) * TC + t - 1)
        hi, low = split(basis(iota((B, 256), 0), zc, COLS))
        for p in range(L):
            chi_ref[p * B : (p + 1) * B, n * 256 : (n + 1) * 256] = hi
            clo_ref[p * B : (p + 1) * B, n * 256 : (n + 1) * 256] = low

    @pl.when(is_parent)
    def _():
        s = TR * row + iota((TR, TC), 0) - off
        s = jnp.where(s < 0, s + ROWS, s)
        for p in range(L):
            x_ref[p] = jnp.where(s < ROWS // 3, 0.0, x_ref[p].astype(F32)).astype(BF16)

    bytes_wait(y_ref, y_recv)
    total = ysrc_ref[...]
    for d in range(7):
        total = total + y_ref[d]
    zsrc_ref[...] = total
    for d in range(1, NZ):
        pltpu.make_async_remote_copy(
            src_ref=zsrc_ref, dst_ref=z_ref.at[d - 1], send_sem=z_send, recv_sem=z_recv,
            device_id=z_peer(d), device_id_type=MESH,
        ).start()

    @pl.when(jnp.logical_not(is_parent))
    def _():
        bytes_wait(gat_ref.at[pl.ds(0, NR - 1)], g_recv)
        v = 2 * TR * zed + iota((2 * TR, 256), 0) - off
        q = iota((2 * TR, 256), 1)
        pick = jnp.where((v == q) | (v + ROWS == q), 1.0, 0.0).astype(BF16)
        for k in range(2):
            rows = dot(pick, gat_ref[:, k].reshape(256, 256)).astype(BF16)
            win_ref[0, k] = rows[:TR]
            win_ref[1, k] = rows[TR:]
        for k in range(2):
            pltpu.make_async_remote_copy(
                src_ref=win_ref.at[k], dst_ref=fed_ref.at[grp, core], send_sem=w_send, recv_sem=w_recv,
                device_id=(NX - 1, 2 * zed + k, col), device_id_type=MESH,
            ).start()

    bytes_wait(z_ref, z_recv)
    total = zsrc_ref[...]
    for d in range(7):
        total = total + z_ref[d]
    all_ref[seat] = drvp_ref[seat] - total
    for d in range(1, 8):
        pltpu.make_async_remote_copy(
            src_ref=all_ref.at[seat], dst_ref=all_ref.at[seat], send_sem=ag_send, recv_sem=ag_recv,
            device_id=seat_peer(d)[1], device_id_type=MESH,
        ).start()
    bytes_wait(all_ref.at[pl.ds(0, 7)], ag_recv)

    hi, low = split(
        jnp.concatenate([all_ref[0:4].reshape(B, 128), all_ref[4:8].reshape(B, 128)], axis=1)
    )
    left = dot(rows3_ref[...], jnp.concatenate([hi, low, hi], axis=0))
    slot = iota((TR, 256), 1) // B
    parts = []
    for l in range(L):
        lev = jnp.where(is_parent, l, lev_ref[l])
        parts.append(jnp.where(slot == lev, left * rate_ref[lev], 0.0))
    lhi, llow = split(jnp.concatenate(parts, axis=0))

    @pl.when(is_parent)
    def _():
        bytes_wait(fed_ref, w_recv)
        for g in range(3):
            for p in range(L):
                cut = (p, slice(None), slice(256 * g, 256 * g + 256))
                x_ref[cut] = x_ref[cut] + fed_ref[g, p // 2, p % 2]

    for n in range(3):
        cut = slice(n * 256, n * 256 + 256)
        inc = dot(lhi, chi_ref[:, cut]) + dot(lhi, clo_ref[:, cut]) + dot(llow, chi_ref[:, cut])
        base = x_ref[:, :, cut].astype(F32)
        out_ref[:, :, cut] = (base + inc.reshape(L, TR, 256)).astype(BF16)

    bytes_wait(rs_ref, rs_send)
    bytes_wait(y_ref, y_send)
    bytes_wait(z_ref, z_send)
    bytes_wait(all_ref.at[pl.ds(0, 7)], ag_send)

    @pl.when(jnp.logical_not(is_parent))
    def _():
        bytes_wait(gat_ref.at[pl.ds(0, NR - 1)], g_send)
        bytes_wait(win_ref, w_send)


def per_device(fields, offset, level_index, nudge_rate, driving):
    smem = pl.BlockSpec(memory_space=pltpu.SMEM)
    vmem = pl.BlockSpec(memory_space=pltpu.VMEM)
    dma = pltpu.SemaphoreType.DMA
    out = pl.pallas_call(
        kernel,
        out_shape=jax.ShapeDtypeStruct((L, TR, TC), BF16),
        in_specs=[pl.BlockSpec(memory_space=pl.ANY), smem, smem, smem, vmem],
        out_specs=vmem,
        scratch_shapes=[
            pltpu.VMEM((L, TR, TC), BF16),
            pltpu.VMEM((TC, 256), BF16),
            pltpu.VMEM((2, L * TR, 128), F32),
            pltpu.VMEM((L, 16, 256), F32),
            pltpu.VMEM((L, 16, 256), BF16),
            pltpu.VMEM((B, TC), BF16),
            pltpu.VMEM((8, 16, 128), F32),
            pltpu.VMEM((7, 16, 128), F32),
            pltpu.VMEM((16, 128), F32),
            pltpu.VMEM((7, 16, 128), F32),
            pltpu.VMEM((16, 128), F32),
            pltpu.VMEM((7, 16, 128), F32),
            pltpu.VMEM((8, 16, 128), F32),
            pltpu.VMEM((NR, 2, 16, 256), BF16),
            pltpu.VMEM((2, 2, TR, 256), BF16),
            pltpu.VMEM((3, 2, 2, TR, 256), BF16),
            pltpu.VMEM((8, 16, 128), F32),
            pltpu.VMEM((TR, 3 * B), BF16),
            pltpu.VMEM((256, TC), BF16),
            pltpu.VMEM((256, TC), BF16),
        ]
        + [dma] * 13,
        compiler_params=pltpu.CompilerParams(collective_id=0, has_side_effects=True),
    )(fields[0], offset, level_index, nudge_rate, driving)
    return out[None]


def solution(mesh):
    spec = P("grp", None, "row", "col")
    return jax.shard_map(
        per_device, mesh=mesh, in_specs=(spec, P(), P(), P(), P()), out_specs=spec, check_vma=False
    )
```

time: 147 us -> 37.2 us (0.25)
  waiting for transfers between devices: 53 us -> 0 us
  starting transfers between devices: 38 us -> 0 us
  Pallas kernels: 0 us -> 34.6 us
  local copies, waits for them, and re-layouts: 34 us -> 1.69 us
  other arithmetic: 17.2 us -> 0 us
  matrix products: 2.96 us -> 0 us
    all_to_all x6 -> x0, waiting for transfers between devices: 53 us -> none  [the longest x4 38 us: sent_to_all(): lax.all_to_all(jnp.broadcast_to(shard[None], (peers, *shard.shape)), axis...]
    all_to_all x6 -> x0, starting transfers between devices: 38 us -> none  [the longest x4 26.5 us: sent_to_all(): lax.all_to_all(jnp.broadcast_to(shard[None], (peers, *shard.shape)), axis...]
    pallas_call x0 -> x1, Pallas kernels: none -> 34.6 us  [per_device(): pl.pallas_call(kernel, out_shape=jax.ShapeDtypeStruct((L, TR, TC), BF16),...]
    convert_element_type x1 -> x0, local copies, waits for them, and re-layouts: 25.9 us -> none  [per_device(): jnp.sum(local_slab.reshape(levels, third_rows, 3, third_cols, 3), axis=(2...]
    reduce_sum x4 -> x0, other arithmetic: 13.3 us -> none  [the longest x1 11.8 us: per_device(): jnp.sum(local_slab.reshape(levels, third_rows, 3, third_cols, 3), axis=(2...]
    dot_general x4 -> x0, matrix products: 2.96 us -> none  [the longest x1 1.49 us: per_device(): jnp.einsum('rn,lnc->lrc', rows_used, spread_cols, precision=lax.Precision...]
    gather x4 -> x0, local copies, waits for them, and re-layouts: 2.4 us -> none  [the longest x1 0.66 us: place_rows(): picked = jnp.take(block_rows, jnp.clip(strip_index, 0, height - 1), axis=1)]
    broadcast_in_dim x4 -> x0, local copies, waits for them, and re-layouts: 2.26 us -> none  [sent_to_all(): jnp.broadcast_to(shard[None], (peers, *shard.shape))]
  transfers between devices with their start and end apart: 6 -> 0, of which waited for: 6 -> 0; matrix products, arithmetic and copies ran while one was open for 2% -> 0% of each run, Pallas kernels for 0% -> 0%
where the time goes in v1:
time: 37.2 us; the launch traced here: 37 us
  Pallas kernels  34.6 us (93%)
  local copies, waits for them, and re-layouts  1.69 us (5%)
  between operations  0.66 us (2%)
    pallas_call x1, Pallas kernels, per_device(): pl.pallas_call(kernel, out_shape=jax.ShapeDtypeStruct((L, TR, TC), BF16),...  34.6 us
    unnamed x1, local copies, waits for them, and re-layouts  1.69 us

profile of v1, /device:TPU:1, one launch (start us, length us, event | category | flops | bytes accessed | tf_op | source)
XLA Modules:
  0.0 37.0 jit_solution(15487358548864246678)
XLA Ops:
  0.7 34.6 %shard_map.55 = bf16[4,48,768]{2,1,0:T(8,128)(2,1)} custom-call(bf16[4,48,768]{2,1,0:T(8,128)(2,1)} %bitcast.3, s32[1]{0:T(128)S(6)} %copy.7.off_ref, s32[4]{0:T(128)} %lev_ref.1, f32[4]{0:T(128)} %rate_ref.1, f32[4,64,64]{2,1,0:T(8,128)} %drv_ref.1), custom_call_target="tpu_custom_call" | custom-call | tf_op jit(solution)/shard_map/pallas_call | solution.py:298
  35.3 1.7 %copy.8 = bf16[1,4,48,768]{3,2,1,0:T(8,128)(2,1)} copy(bf16[1,4,48,768]{3,2,1,0:T(8,128)(2,1)} %bitcast.2) | data formatting | bytes 589824

commit v2 on v1

--- a/solution.py
+++ b/solution.py
@@ -23,6 +23,7 @@
 NY = 8
 NZ = 8
 NR = 16
+FAR_FIRST = (4, 3, 5, 2, 6, 1, 7)
 
 
 def iota(shape, dim):
@@ -63,10 +64,10 @@
 
 
 def kernel(
-    x_hbm, off_ref, lev_ref, rate_ref, drv_ref, out_ref,
-    x_ref, pool_ref, sums_ref, avg_ref, own_ref, colt_ref, part_ref, rs_ref, ysrc_ref, y_ref,
+    x_hbm, off_ref, lev_hbm, rate_hbm, drv_hbm, out_ref,
+    lev_ref, rate_ref, drv_ref, x_ref, pool_ref, sums_ref, avg_ref, own_ref, colt_ref, part_ref, rs_ref, ysrc_ref, y_ref,
     zsrc_ref, z_ref, all_ref, gat_ref, win_ref, fed_ref, drvp_ref, rows3_ref, chi_ref, clo_ref,
-    in_sem, rs_send, rs_recv, y_send, y_recv, z_send, z_recv, ag_send, ag_recv,
+    in_sem, lev_sem, rate_sem, drv_sem, rs_send, rs_recv, y_send, y_recv, z_send, z_recv, ag_send, ag_recv,
     g_send, g_recv, w_send, w_recv,
 ):
     grp = lax.axis_index("grp")
@@ -76,10 +77,14 @@
     core = row % 2
     seat = grp * 2 + core
     is_parent = grp == NX - 1
-    off = off_ref[0]
-
     load = pltpu.make_async_copy(x_hbm, x_ref, in_sem)
     load.start()
+    load_lev = pltpu.make_async_copy(lev_hbm, lev_ref, lev_sem)
+    load_rate = pltpu.make_async_copy(rate_hbm, rate_ref, rate_sem)
+    load_drv = pltpu.make_async_copy(drv_hbm, drv_ref, drv_sem)
+    load_lev.start()
+    load_rate.start()
+    load_drv.start()
 
     barrier = pltpu.get_barrier_semaphore()
 
@@ -96,14 +101,15 @@
     def greet(dev):
         pl.semaphore_signal(barrier, inc=1, device_id=dev, device_id_type=MESH)
 
-    for d in range(1, 8):
+    for d in FAR_FIRST:
         greet(seat_peer(d)[1])
+    for d in FAR_FIRST:
         greet(y_peer(d))
         greet(z_peer(d))
 
     @pl.when(jnp.logical_not(is_parent))
     def _():
-        for d in range(1, 8):
+        for d in FAR_FIRST:
             greet((grp, ((zed + d) % NZ) * 2 + 1 - core, col))
 
     @pl.when(jnp.logical_not(is_parent))
@@ -119,6 +125,8 @@
         xs = 3 * (col * TC + iota((B, TC), 1))
         colt_ref[...] = basis(iota((B, TC), 0), xs, COLS).astype(BF16)
 
+    load_lev.wait()
+    off = off_ref[0]
     load.wait()
 
     def add_part(rowt, proj, rows):
@@ -127,7 +135,9 @@
             both = jnp.concatenate([proj[lo : lo + rows], proj[lo + rows : lo + 2 * rows]], axis=1)
             hi, low = split(both)
             part = dot(rowt, hi) + dot(rowt, low)
-            part_ref[4 * pair : 4 * pair + 4] = part.reshape(4, 16, 128)
+            part = part.reshape(4, 2, 8, 128)
+            for h in range(2):
+                part_ref[h, 4 * pair : 4 * pair + 4] = part[:, h]
 
     @pl.when(jnp.logical_not(is_parent))
     def _():
@@ -163,12 +173,16 @@
 
     pl.semaphore_wait(barrier, jnp.where(is_parent, 21, 28))
 
-    for d in range(1, 8):
-        other, dev = seat_peer(d)
+    def send(src, dst, sems, h, dev):
         pltpu.make_async_remote_copy(
-            src_ref=part_ref.at[other], dst_ref=rs_ref.at[d - 1], send_sem=rs_send, recv_sem=rs_recv,
+            src_ref=src, dst_ref=dst, send_sem=sems[0].at[h], recv_sem=sems[1].at[h],
             device_id=dev, device_id_type=MESH,
         ).start()
+
+    for h in range(2):
+        for d in FAR_FIRST:
+            other, dev = seat_peer(d)
+            send(part_ref.at[h, other], rs_ref.at[h, d - 1], (rs_send, rs_recv), h, dev)
 
     @pl.when(jnp.logical_not(is_parent))
     def _():
@@ -180,26 +194,29 @@
             ).start()
         gat_ref[row] = own_ref[pl.ds(2 * core, 2)]
 
+    load_drv.wait()
+    load_rate.wait()
     for pair in range(2):
         both = jnp.concatenate([drv_ref[2 * pair], drv_ref[2 * pair + 1]], axis=1)
-        drvp_ref[4 * pair : 4 * pair + 4] = (
-            both * (math.sqrt(ROWS * COLS) / (2 * W))
-        ).reshape(4, 16, 128)
+        both = (both * (math.sqrt(ROWS * COLS) / (2 * W))).reshape(4, 2, 8, 128)
+        for h in range(2):
+            drvp_ref[h, 4 * pair : 4 * pair + 4] = both[:, h]
     t = iota((TR, B), 0)
     zr = jnp.where(is_parent, 3 * (TR * row + t), 3 * off + TR * row + t - 1)
     hi, low = split(basis(iota((TR, B), 1), zr, ROWS))
     rows3_ref[...] = jnp.concatenate([hi, hi, low], axis=1)
 
-    bytes_wait(rs_ref, rs_recv)
-    total = part_ref[seat]
-    for d in range(7):
-        total = total + rs_ref[d]
-    ysrc_ref[...] = total
-    for d in range(1, NY):
-        pltpu.make_async_remote_copy(
-            src_ref=ysrc_ref, dst_ref=y_ref.at[d - 1], send_sem=y_send, recv_sem=y_recv,
-            device_id=y_peer(d), device_id_type=MESH,
-        ).start()
+    def summed(own, got, h):
+        total = own
+        for d in range(7):
+            total = total + got[h, d]
+        return total
+
+    for h in range(2):
+        bytes_wait(rs_ref.at[h], rs_recv.at[h])
+        ysrc_ref[h] = summed(part_ref[h, seat], rs_ref, h)
+        for d in FAR_FIRST:
+            send(ysrc_ref.at[h], y_ref.at[h, d - 1], (y_send, y_recv), h, y_peer(d))
 
     for n in range(3):
         t = iota((B, 256), 1) + 256 * n
@@ -216,16 +233,11 @@
         for p in range(L):
             x_ref[p] = jnp.where(s < ROWS // 3, 0.0, x_ref[p].astype(F32)).astype(BF16)
 
-    bytes_wait(y_ref, y_recv)
-    total = ysrc_ref[...]
-    for d in range(7):
-        total = total + y_ref[d]
-    zsrc_ref[...] = total
-    for d in range(1, NZ):
-        pltpu.make_async_remote_copy(
-            src_ref=zsrc_ref, dst_ref=z_ref.at[d - 1], send_sem=z_send, recv_sem=z_recv,
-            device_id=z_peer(d), device_id_type=MESH,
-        ).start()
+    for h in range(2):
+        bytes_wait(y_ref.at[h], y_recv.at[h])
+        zsrc_ref[h] = summed(ysrc_ref[h], y_ref, h)
+        for d in FAR_FIRST:
+            send(zsrc_ref.at[h], z_ref.at[h, d - 1], (z_send, z_recv), h, z_peer(d))
 
     @pl.when(jnp.logical_not(is_parent))
     def _():
@@ -243,21 +255,17 @@
                 device_id=(NX - 1, 2 * zed + k, col), device_id_type=MESH,
             ).start()
 
-    bytes_wait(z_ref, z_recv)
-    total = zsrc_ref[...]
-    for d in range(7):
-        total = total + z_ref[d]
-    all_ref[seat] = drvp_ref[seat] - total
-    for d in range(1, 8):
-        pltpu.make_async_remote_copy(
-            src_ref=all_ref.at[seat], dst_ref=all_ref.at[seat], send_sem=ag_send, recv_sem=ag_recv,
-            device_id=seat_peer(d)[1], device_id_type=MESH,
-        ).start()
-    bytes_wait(all_ref.at[pl.ds(0, 7)], ag_recv)
-
-    hi, low = split(
-        jnp.concatenate([all_ref[0:4].reshape(B, 128), all_ref[4:8].reshape(B, 128)], axis=1)
-    )
+    for h in range(2):
+        bytes_wait(z_ref.at[h], z_recv.at[h])
+        all_ref[h, seat] = drvp_ref[h, seat] - summed(zsrc_ref[h], z_ref, h)
+        for d in FAR_FIRST:
+            mine = all_ref.at[h, seat]
+            send(mine, mine, (ag_send, ag_recv), h, seat_peer(d)[1])
+    for h in range(2):
+        bytes_wait(all_ref.at[h, pl.ds(0, 7)], ag_recv.at[h])
+
+    whole = jnp.stack([all_ref[0], all_ref[1]], axis=1).reshape(2, B, 128)
+    hi, low = split(jnp.concatenate([whole[0], whole[1]], axis=1))
     left = dot(rows3_ref[...], jnp.concatenate([hi, low, hi], axis=0))
     slot = iota((TR, 256), 1) // B
     parts = []
@@ -280,10 +288,11 @@
         base = x_ref[:, :, cut].astype(F32)
         out_ref[:, :, cut] = (base + inc.reshape(L, TR, 256)).astype(BF16)
 
-    bytes_wait(rs_ref, rs_send)
-    bytes_wait(y_ref, y_send)
-    bytes_wait(z_ref, z_send)
-    bytes_wait(all_ref.at[pl.ds(0, 7)], ag_send)
+    for h in range(2):
+        bytes_wait(rs_ref.at[h], rs_send.at[h])
+        bytes_wait(y_ref.at[h], y_send.at[h])
+        bytes_wait(z_ref.at[h], z_send.at[h])
+        bytes_wait(all_ref.at[h, pl.ds(0, 7)], ag_send.at[h])
 
     @pl.when(jnp.logical_not(is_parent))
     def _():
@@ -292,38 +301,44 @@
 
 
 def per_device(fields, offset, level_index, nudge_rate, driving):
-    smem = pl.BlockSpec(memory_space=pltpu.SMEM)
-    vmem = pl.BlockSpec(memory_space=pltpu.VMEM)
+    anywhere = pl.BlockSpec(memory_space=pltpu.HBM)
     dma = pltpu.SemaphoreType.DMA
     out = pl.pallas_call(
         kernel,
-        out_shape=jax.ShapeDtypeStruct((L, TR, TC), BF16),
-        in_specs=[pl.BlockSpec(memory_space=pl.ANY), smem, smem, smem, vmem],
-        out_specs=vmem,
+        out_shape=pltpu.VMEM((L, TR, TC), BF16),
+        in_specs=[anywhere, pl.BlockSpec(memory_space=pltpu.SMEM)] + [anywhere] * 3,
+        out_specs=pl.BlockSpec(memory_space=pltpu.VMEM),
         scratch_shapes=[
+            pltpu.SMEM((L,), I32),
+            pltpu.SMEM((L,), F32),
+            pltpu.VMEM((L, B, B), F32),
             pltpu.VMEM((L, TR, TC), BF16),
             pltpu.VMEM((TC, 256), BF16),
             pltpu.VMEM((2, L * TR, 128), F32),
             pltpu.VMEM((L, 16, 256), F32),
             pltpu.VMEM((L, 16, 256), BF16),
             pltpu.VMEM((B, TC), BF16),
-            pltpu.VMEM((8, 16, 128), F32),
-            pltpu.VMEM((7, 16, 128), F32),
-            pltpu.VMEM((16, 128), F32),
-            pltpu.VMEM((7, 16, 128), F32),
-            pltpu.VMEM((16, 128), F32),
-            pltpu.VMEM((7, 16, 128), F32),
-            pltpu.VMEM((8, 16, 128), F32),
+            pltpu.VMEM((2, 8, 8, 128), F32),
+            pltpu.VMEM((2, 7, 8, 128), F32),
+            pltpu.VMEM((2, 8, 128), F32),
+            pltpu.VMEM((2, 7, 8, 128), F32),
+            pltpu.VMEM((2, 8, 128), F32),
+            pltpu.VMEM((2, 7, 8, 128), F32),
+            pltpu.VMEM((2, 8, 8, 128), F32),
             pltpu.VMEM((NR, 2, 16, 256), BF16),
             pltpu.VMEM((2, 2, TR, 256), BF16),
             pltpu.VMEM((3, 2, 2, TR, 256), BF16),
-            pltpu.VMEM((8, 16, 128), F32),
+            pltpu.VMEM((2, 8, 8, 128), F32),
             pltpu.VMEM((TR, 3 * B), BF16),
             pltpu.VMEM((256, TC), BF16),
             pltpu.VMEM((256, TC), BF16),
         ]
-        + [dma] * 13,
-        compiler_params=pltpu.CompilerParams(collective_id=0, has_side_effects=True),
+        + [dma] * 4
+        + [dma((2,))] * 8
+        + [dma] * 4,
+        compiler_params=pltpu.CompilerParams(
+            collective_id=0, has_side_effects=True
+        ),
     )(fields[0], offset, level_index, nudge_rate, driving)
     return out[None]
 

time: 37.2 us -> 33.8 us (0.909)
  Pallas kernels: 34.6 us -> 32.3 us
  local copies, waits for them, and re-layouts: 1.69 us -> 0.72 us
    pallas_call x1, Pallas kernels: 34.6 us -> 32.3 us  [per_device(): pl.pallas_call(kernel, out_shape=pltpu.VMEM((L, TR, TC), BF16), in_specs=...]
    unnamed x1, local copies, waits for them, and re-layouts: 1.69 us -> 0.72 us
where the time goes in v2:
time: 33.8 us; the launch traced here: 33.6 us
  Pallas kernels  32.3 us (96%)
  local copies, waits for them, and re-layouts  0.72 us (2%)
  between operations  0.66 us (2%)
    pallas_call x1, Pallas kernels, per_device(): pl.pallas_call(kernel, out_shape=pltpu.VMEM((L, TR, TC), BF16), in_specs=...  32.3 us
    unnamed x1, local copies, waits for them, and re-layouts  0.72 us

profile of v2, /device:TPU:1, one launch (start us, length us, event | category | flops | bytes accessed | tf_op | source)
XLA Modules:
  0.0 33.6 jit_solution(15450088638810936937)
XLA Ops:
  0.7 32.3 %shard_map.55 = bf16[4,48,768]{2,1,0:T(8,128)(2,1)S(1)} custom-call(bf16[4,48,768]{2,1,0:T(8,128)(2,1)} %bitcast.3, s32[1]{0:T(128)S(6)} %copy.8.off_ref, s32[4]{0:T(128)} %lev_hbm.1, f32[4]{0:T(128)} %rate_hbm.1, f32[4,64,64]{2,1,0:T(8,128)} %drv_hbm.1), custom_call_target="tpu_custom_call" | custom-call | tf_op jit(solution)/shard_map/pallas_call | solution.py:306
  32.9 0.7 %copy.7 = bf16[1,4,48,768]{3,2,1,0:T(8,128)(2,1)} copy(bf16[1,4,48,768]{3,2,1,0:T(8,128)(2,1)S(1)} %bitcast.2) | data formatting | bytes 589824
